TPU v7x, 32 devices: a whole 2x2x4 slice. The times are simulated.
32 devices in a mesh: grp: 8 (over z, x), row: 4 (over y, core).
Axes of the slice: x: 2, y: 2, z: 4, core: 2. Of those that a mesh axis runs over, the one named last changes fastest.
Arguments:
- gll_state: float32 [8, 32, 16, 4096], P(None, None, None, ('grp', 'row')), may hold values from -6 to 6
- metric: float32 [16, 4096], P(None, ('grp', 'row')), may hold values from 0.7 to 1.4
- phys_owner: int32 [4096, 4, 1], P(('grp', 'row')), may hold values from 0 to 7; in each aligned block of 512 rows (0 to 511, 512 to 1023, ..., all dimensions but the last counted through in order) at most 128 rows name the same one
- neighbours: int32 [4, 4096], P(None, ('grp', 'row')), may hold values from 0 to 4095, as said below
- phys_rate: float32 [32, 32768], P(None, ('grp', 'row')), may hold values from 0.2 to 2
- phys_forcing: float32 [32, 32768], P(None, ('grp', 'row')), may hold values from -6 to 6
- field_mix: float32 [8, 8], replicated, may hold values from -2 to 2
Outputs:
- gll_tend: float32 [8, 32, 16, 4096], P(None, None, None, ('grp', 'row'))
Inputs may be any that keep to these rules, and one draw needn't show every extreme that they name: `phys_owner`: in the 512 rows of one device, no owner is named more than 128 times, and some owner reaches 128. `neighbours`: rows 0 and 1 of element e are e - 1 and e + 1, cyclically over 4096 elements; rows 2 and 3 lie 2 to 32 positions before and after e, cyclically, and some element has a neighbour exactly 32 positions away.
All inputs are finite; a program needn't handle non-finite values.
Results may differ from a plain program's by a relative error of at most 0.000094.
Values sent between devices are 32-bit elements; how exact they have to be, the bound alone decides.
No kernel may reach another device: no remote copies, remote signals or barrier semaphores. Data moves between devices by JAX's collectives and lax.ppermute only.
A program may use at most 64 MiB of HBM per device.

v0:
```python
import jax
import jax.numpy as jnp
import numpy as np
from jax import lax
from jax.sharding import PartitionSpec as P

HALO = 32


def padded_2(cells, sides, width):
    for axis, dim in sides:
        count = lax.axis_size(axis)
        head = lax.slice_in_dim(cells, 0, width, axis=dim)
        tail = lax.slice_in_dim(cells, cells.shape[dim] - width, cells.shape[dim], axis=dim)
        cells = jnp.concatenate(
            [
                lax.ppermute(tail, axis, [(i, (i + 1) % count) for i in range(count)]),
                cells,
                lax.ppermute(head, axis, [((i + 1) % count, i) for i in range(count)]),
            ],
            axis=dim,
        )
    return cells


def lagrange_value(gll_nodes, node_index, point):
    value = 1.0
    for other_index in range(4):
        if other_index != node_index:
            value = (
                value
                * (point - gll_nodes[other_index])
                / (gll_nodes[node_index] - gll_nodes[other_index])
            )
    return value


def remap_tables():
    gll_nodes = np.array([-1.0, -1.0 / np.sqrt(5.0), 1.0 / np.sqrt(5.0), 1.0])
    offset = 0.5 / np.sqrt(3.0)
    halves = np.zeros((2, 4))
    for node_index in range(4):
        left_sum = lagrange_value(gll_nodes, node_index, -0.5 - offset) + lagrange_value(
            gll_nodes, node_index, -0.5 + offset
        )
        right_sum = lagrange_value(gll_nodes, node_index, 0.5 - offset) + lagrange_value(
            gll_nodes, node_index, 0.5 + offset
        )
        halves[0, node_index] = 0.5 * left_sum
        halves[1, node_index] = 0.5 * right_sum
    cell_weights = (halves[None, :, None, :] * halves[:, None, :, None]).reshape(4, 16)
    interp_cols = np.stack([0.5 - gll_nodes, 0.5 + gll_nodes], axis=1)
    cell_to_node = (interp_cols[None, :, None, :] * interp_cols[:, None, :, None]).reshape(16, 4)
    node_x = np.tile(gll_nodes, 4)
    node_y = np.repeat(gll_nodes, 4)
    slope_weights = 0.5 * np.stack(
        [
            np.maximum(0.0, -node_x),
            np.maximum(0.0, node_x),
            np.maximum(0.0, -node_y),
            np.maximum(0.0, node_y),
        ],
        axis=1,
    )
    return (
        jnp.asarray(cell_weights, jnp.float32),
        jnp.asarray(cell_to_node, jnp.float32),
        jnp.asarray(slope_weights, jnp.float32),
    )


def to_cells(gll_state, metric):
    cell_weights, cell_to_node, slope_weights = remap_tables()
    weighted = cell_weights[:, :, None] * metric[None, :, :]
    cell_area = jnp.sum(weighted, axis=1)
    cell_mass = jnp.einsum("cne,flne->flce", weighted, gll_state, precision=lax.Precision.HIGHEST)
    return cell_mass / cell_area[None, None]


def physics(cell_values, relax_rate, forcing, field_mix):
    mixed_fields = jnp.einsum(
        "fg,g...->f...", field_mix, cell_values, precision=lax.Precision.HIGHEST
    )
    return relax_rate[None] * jnp.tanh(mixed_fields + forcing[None])


def to_nodes(tendency, neighbour_means):
    cell_weights, cell_to_node, slope_weights = remap_tables()
    own_mean = jnp.mean(tendency, axis=2)
    reconstructed = jnp.einsum(
        "nc,flce->flne", cell_to_node, tendency, precision=lax.Precision.HIGHEST
    )
    reconstructed = reconstructed + jnp.einsum(
        "nk,flke->flne",
        slope_weights,
        neighbour_means - own_mean[:, :, None],
        precision=lax.Precision.HIGHEST,
    )
    lower_bound = jnp.minimum(jnp.min(tendency, axis=2), jnp.min(neighbour_means, axis=2))
    upper_bound = jnp.maximum(jnp.max(tendency, axis=2), jnp.max(neighbour_means, axis=2))
    return jnp.clip(reconstructed, lower_bound[:, :, None], upper_bound[:, :, None])


def on_device(gll_state, metric, phys_owner, neighbours, phys_rate, phys_forcing, field_mix):
    field_count, level_count, node_count, elem_count = gll_state.shape
    grp_size = lax.axis_size("grp")
    row_size = lax.axis_size("row")
    capacity = phys_rate.shape[1] // grp_size
    cell_values = to_cells(gll_state, metric)
    column_cells = cell_values.transpose(0, 1, 3, 2).reshape(
        field_count, level_count, 4 * elem_count
    )
    owner_grp = phys_owner[:, :, 0].reshape(4 * elem_count)
    onehot = (owner_grp[:, None] == jnp.arange(grp_size, dtype=jnp.int32)[None, :]).astype(
        jnp.int32
    )
    slot_rank = jnp.sum((jnp.cumsum(onehot, axis=0) - onehot) * onehot, axis=1)
    target = owner_grp * capacity + slot_rank
    rate_slots, forcing_slots = (
        lax.all_to_all(
            phys_rate.reshape(level_count, grp_size, capacity),
            "grp",
            split_axis=1,
            concat_axis=1,
            tiled=True,
        ),
        lax.all_to_all(
            phys_forcing.reshape(level_count, grp_size, capacity),
            "grp",
            split_axis=1,
            concat_axis=1,
            tiled=True,
        ),
    )
    relax_rate = rate_slots.reshape(level_count, grp_size * capacity)[:, target]
    forcing = forcing_slots.reshape(level_count, grp_size * capacity)[:, target]
    column_tend = physics(column_cells, relax_rate, forcing, field_mix)
    tendency = column_tend.reshape(field_count, level_count, elem_count, 4).transpose(0, 1, 3, 2)
    own_mean = jnp.mean(tendency, axis=2).reshape(field_count * level_count, elem_count)
    padded = padded_2(own_mean, ((("grp", "row"), 1),), HALO)
    total_elems = elem_count * grp_size * row_size
    first_elem = (lax.axis_index("grp") * row_size + lax.axis_index("row")) * elem_count
    local_index = (neighbours - first_elem + HALO) % total_elems
    neighbour_means = jnp.take(padded, local_index, axis=1).reshape(
        field_count, level_count, 4, elem_count
    )
    return to_nodes(tendency, neighbour_means)


def solution(mesh):
    in_specs = (
        P(None, None, None, ("grp", "row")),
        P(None, ("grp", "row")),
        P(("grp", "row"), None, None),
        P(None, ("grp", "row")),
        P(None, ("grp", "row")),
        P(None, ("grp", "row")),
        P(),
    )
    out_specs = P(None, None, None, ("grp", "row"))
    return jax.shard_map(
        on_device, mesh=mesh, in_specs=in_specs, out_specs=out_specs, check_vma=False
    )
```

profile of v0, /device:TPU:0, one launch (start us, length us, event | category | flops | bytes accessed | tf_op | source)
XLA Modules:
  0.0 66.3 jit_solution(11681408883932094924)
XLA Ops:
  0.0 0.9 %copy-done = f32[32,1024]{1,0:T(8,128)S(1)} copy-done((f32[32,1024]{1,0:T(8,128)S(1)}, f32[32,1024]{1,0:T(8,128)}, u32[]{:S(2)}) %copy-start) | copy-done | bytes 131096
  0.9 0.7 copy_bitcast_fusion
  1.6 7.3 %all-to-all-start.1 = ((f32[32,8,128]{2,0,1:T(8,128)}), f32[32,8,128]{2,0,1:T(8,128)S(1)}, u32[]{:S(2)}, u32[]{:S(2)}) async-start(f32[32,8,128]{2,0,1:T(8,128)} %copy_bitcast_fusion), calls=%async_computation.1 | async-start | bytes 262144 | tf_op jit(solution)/shard_map/all_to_all | solution.py:127
  8.8 0.7 %broadcast_multiply_fusion.1 = s32[128,4,1]{0,2,1:T(1,128)S(1)} fusion(s32[128,4,1]{0,2,1:T(1,128)} %param.12), kind=kLoop, calls=%fused_computation.39 | loop fusion | flops 512 | bytes 4096 | tf_op jit(solution)/shard_map/mul | solution.py:118
  9.5 0.8 %copy.91 = s32[128,4,1]{1,0,2:T(8,128)S(1)} copy(s32[128,4,1]{0,2,1:T(1,128)} %param.12) | data formatting | bytes 4096 | tf_op args[2]
  10.6 8.4 %copy.95 = f32[8,32,16,128]{1,2,0,3:T(8,128)} copy(f32[8,32,16,128]{3,2,1,0:T(8,128)} %param.10) | data formatting | bytes 4194304 | tf_op args[0]
  19.3 1.1 %reduce-window.6 = s32[8,4,128]{2,0,1:T(8,128)S(1)} reduce-window(s32[8,4,128]{2,0,1:T(8,128)S(1)} %fusion.10, s32[]{:T(128)} %constant.29.clone.1), window={size=1x1x128 pad=0_0x0_0x127_0}, to_apply=%region_0.0 | reduce-window | flops 520192 | bytes 32772 | tf_op jit(solution)/shard_map/reduce-window
  20.4 0.2 slice_reduce_fusion
  20.7 0.2 multiply_reduce_fusion
  20.9 7.6 %divide_bitcast_fusion = f32[8,32,128,4]{1,3,0,2:T(4,128)} fusion(f32[8,32,16,128]{1,2,0,3:T(8,128)} %copy.95, f32[128,4]{1,0:T(8,128)S(1)} %bitcast.87, f32[16,128]{0,1:T(8,128)S(1)} %copy.94, f32[4,16]{1,0:T(4,128)S(1)} %copy-done.6), kind=kOutput, calls=%fused_computation.4 | convolution fusion | flops 25305088 | bytes 2631936 | tf_op jit(solution)/shard_map/cne,flne->flce/dot_general | solution.py:76
  28.6 0.6 copy_bitcast_fusion.1
  29.3 6.0 %all-to-all-start = ((f32[32,8,128]{2,0,1:T(8,128)}), f32[32,8,128]{2,0,1:T(8,128)S(1)}, u32[]{:S(2)}, u32[]{:S(2)}) async-start(f32[32,8,128]{2,0,1:T(8,128)} %copy_bitcast_fusion.1), calls=%async_computation | async-start | bytes 262144 | tf_op jit(solution)/shard_map/all_to_all | solution.py:120
  35.3 1.8 %copy.96 = f32[8,32,128,4]{1,0,3,2:T(8,128)S(1)} copy(f32[8,32,128,4]{1,3,0,2:T(4,128)} %divide_bitcast_fusion) | data formatting | bytes 1048576 | tf_op jit(solution)/shard_map/div | solution.py:77
  37.1 0.9 %copy.97 = f32[8,32,512]{2,0,1:T(8,128)S(1)} copy(f32[8,32,512]{1,0,2:T(8,128)S(1)} %bitcast.77) | data formatting | bytes 1048576 | tf_op jit(solution)/shard_map/reshape | solution.py:110
  38.2 1.0 %gather_fusion.1 = f32[512,32]{1,0:T(8,128)S(1)} fusion(f32[32,1024]{0,1:T(8,128)S(1)} %bitcast.81, s32[1024]{0:T(1024)S(1)} %pad_clamp_fusion.1), kind=kCustom, calls=%fused_computation.1 | custom fusion | bytes 133120 | tf_op jit(solution)/shard_map/gather | solution.py:136
  39.4 3.2 %all-to-all-done = f32[32,8,128]{2,0,1:T(8,128)S(1)} async-done(((f32[32,8,128]{2,0,1:T(8,128)}), f32[32,8,128]{2,0,1:T(8,128)S(1)}, u32[]{:S(2)}, u32[]{:S(2)}) %all-to-all-start) | async-done | bytes 131104 | tf_op jit(solution)/shard_map/all_to_all | solution.py:120
  42.8 1.0 %gather_fusion = f32[512,32]{1,0:T(8,128)S(1)} fusion(f32[32,1024]{0,1:T(8,128)S(1)} %bitcast.79, s32[1024]{0:T(1024)S(1)} %pad_clamp_fusion.1), kind=kCustom, calls=%fused_computation | custom fusion | bytes 133120 | tf_op jit(solution)/shard_map/gather | solution.py:135
  44.0 0.6 fusion.2
  44.6 0.8 %copy.101 = f32[8,32,512]{1,0,2:T(8,128)S(1)} copy(f32[8,32,512]{2,0,1:T(8,128)S(1)} %fusion.2) | data formatting | bytes 1048576 | tf_op jit(solution)/shard_map/mul | solution.py:84
  45.4 1.7 %bitcast_reduce_fusion.2 = (f32[8,32,128]{1,0,2:T(8,128)S(1)}, f32[8,32,128]{1,0,2:T(8,128)}, f32[8,32,128]{1,0,2:T(8,128)S(1)}) fusion(f32[8,32,512]{1,0,2:T(8,128)S(1)} %copy.101), kind=kLoop, calls=%fused_computation.42 | loop fusion | flops 294912 | bytes 917504 | tf_op jit(solution)/shard_map/reduce_max | solution.py:100
  47.1 2.1 %copy.113 = f32[8,32,4,128]{3,2,1,0:T(4,128)} copy(f32[8,32,4,128]{1,0,2,3:T(8,128)S(1)} %bitcast.76) | data formatting | bytes 1048576 | tf_op jit(solution)/shard_map/transpose | solution.py:138
  49.1 1.2 %copy.102 = f32[8,32,128]{2,1,0:T(8,128)S(1)} copy(f32[8,32,128]{1,0,2:T(8,128)} %get-tuple-element.6) | data formatting | bytes 262144 | tf_op jit(solution)/shard_map/reduce_sum | solution.py:139
  50.5 0.6 fusion.13
  51.1 0.8 %collective-permute-start.1 = (f32[256,32]{0,1:T(8,128)}, f32[256,32]{0,1:T(8,128)}, u32[]{:S(2)}, u32[]{:S(2)}) collective-permute-start(f32[256,32]{0,1:T(8,128)} %get-tuple-element.13), channel_id=1, source_target_pairs={{1,0},{2,1},{3,2},{4,3},{5,4},{6,5},{7,6},{8,7},{9,8},{10,9},{11,1... | collective-permute-start | bytes 98312 | tf_op jit(solution)/shard_map/ppermute | solution.py:19
  51.9 2.9 %fusion.14 = f32[8,32,128,16]{2,3,1,0:T(8,128)S(1)} fusion(f32[8,32,4,128]{3,2,1,0:T(4,128)} %copy.113, f32[16,4,1,1]{0,1,3,2:T(4,128)S(1)} %copy-done.8), kind=kOutput, calls=%fused_computation.44 | convolution fusion | flops 25165824 | bytes 2621696 | tf_op jit(solution)/shard_map/nc,flce->flne/dot_general | solution.py:90
  54.8 0.9 %copy.112 = f32[8,32,128]{2,1,0:T(8,128)} copy(f32[8,32,128]{1,0,2:T(8,128)S(1)} %get-tuple-element.7) | data formatting | bytes 262144 | tf_op jit(solution)/shard_map/reduce_min | solution.py:99
  55.6 0.8 %copy.109 = f32[8,32,128]{2,1,0:T(8,128)} copy(f32[8,32,128]{1,0,2:T(8,128)S(1)} %get-tuple-element.5) | data formatting | bytes 262144 | tf_op jit(solution)/shard_map/reduce_max | solution.py:100
  56.5 2.7 %collective-permute-done = f32[256,32]{0,1:T(8,128)} collective-permute-done((f32[256,32]{0,1:T(8,128)}, f32[256,32]{0,1:T(8,128)}, u32[]{:S(2)}, u32[]{:S(2)}) %collective-permute-start) | collective-permute-done | bytes 32800 | tf_op jit(solution)/shard_map/ppermute | solution.py:17
  59.1 0.8 %pad_maximum_fusion = f32[256,192]{0,1:T(8,128)S(1)} fusion(f32[256,32]{0,1:T(8,128)} %collective-permute-done.1, f32[256,128]{0,1:T(8,128)S(1)} %copy.103, f32[256,32]{0,1:T(8,128)} %collective-permute-done), kind=kLoop, calls=%fused_computation.16 | loop fusion | flops 98304 | bytes 393216 | tf_op jit(solution)/shard_map/concatenate | solution.py:15
  59.9 1.6 %gather_fusion.2 = f32[512,256]{1,0:T(8,128)S(1)} fusion(f32[256,192]{0,1:T(8,128)S(1)} %pad_maximum_fusion, s32[1024]{0:T(1024)S(1)} %pad_clamp_fusion), kind=kCustom, calls=%fused_computation.2 | custom fusion | bytes 1050624 | tf_op jit(solution)/shard_map/jit(_take)/gather | solution.py:144
  61.8 0.9 %min.23 = f32[8,32,128]{2,1,0:T(8,128)S(1)} minimum(f32[8,32,128]{2,1,0:T(8,128)} %copy.112, f32[8,32,128]{2,1,0:T(8,128)S(1)} %bitcast.84) | non-fusion elementwise | flops 32768 | bytes 393216 | tf_op jit(solution)/shard_map/min | solution.py:99
  62.8 3.4 %minimum_bitcast_fusion = f32[8,32,16,128]{3,2,1,0:T(8,128)} fusion(f32[8,32,128,16]{2,3,1,0:T(8,128)S(1)} %fusion.14, f32[16,4,1,1]{0,1,3,2:T(4,128)S(1)} %copy-done.5, f32[8,32,128]{2,1,0:T(8,128)S(1)} %min.23, f32[8,32,128]{2,1,0:T(8,128)S(1)} %max.20, f32[8,32,4,128]{3,1,0,2:T(8,128)S(1)} %select_subtract_fusion), kind=kOutput, calls=%fused_computation.3 | convolution fusion | flops 26738688 | bytes 4980992 | tf_op jit(solution)/shard_map/nk,flke->flne/dot_general | solution.py:93
  (43 shorter events, 1.8 us)
Async XLA Ops:
  0.0 0.9 %copy-start = (f32[32,1024]{1,0:T(8,128)S(1)}, f32[32,1024]{1,0:T(8,128)}, u32[]{:S(2)}) copy-start(f32[32,1024]{1,0:T(8,128)} %param.15) | copy-start | bytes 393220
  1.6 27.7 %all-to-all-start.1 = ((f32[32,8,128]{2,0,1:T(8,128)}), f32[32,8,128]{2,0,1:T(8,128)S(1)}, u32[]{:S(2)}, u32[]{:S(2)}) async-start(f32[32,8,128]{2,0,1:T(8,128)} %copy_bitcast_fusion), calls=%async_computation.1 | async-start | bytes 262144 | tf_op jit(solution)/shard_map/all_to_all | solution.py:127
  10.5 8.4 %copy-start.3 = (f32[16,128]{1,0:T(8,128)S(1)}, f32[16,128]{1,0:T(8,128)}, u32[]{:S(2)}) copy-start(f32[16,128]{1,0:T(8,128)} %param.11) | copy-start | bytes 24580
  10.6 10.1 %copy-start.6 = (f32[4,16]{1,0:T(4,128)S(1)}, f32[4,16]{1,0:T(4,128)}, u32[]{:S(2)}) copy-start(f32[4,16]{1,0:T(4,128)} %constant.69.clone) | copy-start | bytes 772
  20.9 7.7 %copy-start.2 = (f32[32,1024]{1,0:T(8,128)S(1)}, f32[32,1024]{1,0:T(8,128)}, u32[]{:S(2)}) copy-start(f32[32,1024]{1,0:T(8,128)} %param.14) | copy-start | bytes 393220
  20.9 14.3 %copy-start.7 = (s32[4,128]{1,0:T(4,128)S(1)}, s32[4,128]{1,0:T(4,128)}, u32[]{:S(2)}) copy-start(s32[4,128]{1,0:T(4,128)} %param.13) | copy-start | bytes 6148
  29.3 13.3 %all-to-all-start = ((f32[32,8,128]{2,0,1:T(8,128)}), f32[32,8,128]{2,0,1:T(8,128)S(1)}, u32[]{:S(2)}, u32[]{:S(2)}) async-start(f32[32,8,128]{2,0,1:T(8,128)} %copy_bitcast_fusion.1), calls=%async_computation | async-start | bytes 262144 | tf_op jit(solution)/shard_map/all_to_all | solution.py:120
  38.0 6.0 %copy-start.4 = (f32[8,8]{1,0:T(8,128)S(1)}, f32[8,8]{1,0:T(8,128)}, u32[]{:S(2)}) copy-start(f32[8,8]{1,0:T(8,128)} %param.16) | copy-start | bytes 772
  47.1 4.8 %copy-start.8 = (f32[16,4,1,1]{0,1,3,2:T(4,128)S(1)}, f32[16,4,1,1]{0,1,3,2:T(4,128)}, u32[]{:S(2)}) copy-start(f32[16,4,1,1]{0,1,3,2:T(4,128)} %constant.72) | copy-start | bytes 772
  51.1 5.4 %collective-permute-start.1 = (f32[256,32]{0,1:T(8,128)}, f32[256,32]{0,1:T(8,128)}, u32[]{:S(2)}, u32[]{:S(2)}) collective-permute-start(f32[256,32]{0,1:T(8,128)} %get-tuple-element.13), channel_id=1, source_target_pairs={{1,0},{2,1},{3,2},{4,3},{5,4},{6,5},{7,6},{8,7},{9,8},{10,9},{11,1... | collective-permute-start | bytes 98312 | tf_op jit(solution)/shard_map/ppermute | solution.py:19
  51.9 7.3 %collective-permute-start = (f32[256,32]{0,1:T(8,128)}, f32[256,32]{0,1:T(8,128)}, u32[]{:S(2)}, u32[]{:S(2)}) collective-permute-start(f32[256,32]{0,1:T(8,128)} %get-tuple-element.12), channel_id=1, source_target_pairs={{0,1},{1,2},{2,3},{3,4},{4,5},{5,6},{6,7},{7,8},{8,9},{9,10},{10,1... | collective-permute-start | bytes 98312 | tf_op jit(solution)/shard_map/ppermute | solution.py:17
  61.5 1.3 %copy-start.1 = (f32[8,32,128]{2,1,0:T(8,128)S(1)}, f32[8,32,128]{2,1,0:T(8,128)}, u32[]{:S(2)}) copy-start(f32[8,32,128]{2,1,0:T(8,128)} %copy.109) | copy-start | bytes 393220
  61.5 1.3 %copy-start.5 = (f32[16,4,1,1]{0,1,3,2:T(4,128)S(1)}, f32[16,4,1,1]{0,1,3,2:T(4,128)}, u32[]{:S(2)}) copy-start(f32[16,4,1,1]{0,1,3,2:T(4,128)} %constant.73) | copy-start | bytes 772
where the time goes:
time: 66.8 us; the launch traced here: 66.3 us
  local copies, waits for them, and re-layouts  25.8 us (39%)
  matrix products  14.5 us (22%)
  starting transfers between devices  14 us (21%)
  waiting for transfers between devices  5.89 us (9%)
  other arithmetic  5.73 us (9%)
    unnamed x21, local copies, waits for them, and re-layouts  10.2 us
    dot_general x1, matrix products, to_cells(): jnp.einsum('cne,flne->flce', weighted, gll_state, precision=lax.Precision...  7.56 us
    all_to_all x1, starting transfers between devices, on_device(): lax.all_to_all(phys_forcing.reshape(level_count, grp_size, capacity), 'gr...  7.28 us
    all_to_all x1, starting transfers between devices, on_device(): lax.all_to_all(phys_rate.reshape(level_count, grp_size, capacity), 'grp',...  6 us
    dot_general x1, matrix products, to_nodes(): jnp.einsum('nk,flke->flne', slope_weights, neighbour_means - own_mean[:,...  3.44 us
    all_to_all x1, waiting for transfers between devices, on_device(): lax.all_to_all(phys_rate.reshape(level_count, grp_size, capacity), 'grp',...  3.24 us
    dot_general x1, matrix products, to_nodes(): jnp.einsum('nc,flce->flne', cell_to_node, tendency, precision=lax.Precisi...  2.87 us
    ppermute x1, waiting for transfers between devices, padded_2(): lax.ppermute(tail, axis, [(i, (i + 1) % count) for i in range(count)])  2.65 us
  transfers between devices with their start and end apart: 4, of which 2 were waited for; matrix products, arithmetic and copies ran while one was open for 44% of the time, Pallas kernels for 0%

commit v1 on v0

--- a/solution.py
+++ b/solution.py
@@ -5,6 +5,15 @@
 from jax.sharding import PartitionSpec as P
 
 HALO = 32
+
+
+def switch_the_inputs(block_in, along_dim, row_dim):
+    return jnp.concatenate(
+        lax.all_to_all(
+            jnp.stack(jnp.split(block_in, lax.axis_size("grp"), axis=along_dim)), "grp", 0, 0
+        ),
+        axis=row_dim,
+    )
 
 
 def padded_2(cells, sides, width):
@@ -124,13 +133,7 @@
             concat_axis=1,
             tiled=True,
         ),
-        lax.all_to_all(
-            phys_forcing.reshape(level_count, grp_size, capacity),
-            "grp",
-            split_axis=1,
-            concat_axis=1,
-            tiled=True,
-        ),
+        switch_the_inputs(phys_forcing.reshape(level_count, grp_size, capacity), 1, 1),
     )
     relax_rate = rate_slots.reshape(level_count, grp_size * capacity)[:, target]
     forcing = forcing_slots.reshape(level_count, grp_size * capacity)[:, target]

time: 66.8 us -> 71.1 us (1.064)
  local copies, waits for them, and re-layouts: 25.8 us -> 30.1 us
    unnamed x21 -> x27, local copies, waits for them, and re-layouts: 10.2 us -> 14.5 us
  transfers between devices with their start and end apart: 4 -> 4, of which waited for: 2 -> 2; matrix products, arithmetic and copies ran while one was open for 44% -> 41% of each run, Pallas kernels for 0% -> 0%
where the time goes in v1:
time: 71.1 us; the launch traced here: 70.5 us
  local copies, waits for them, and re-layouts  30.1 us (42%)
  matrix products  14.4 us (20%)
  starting transfers between devices  14 us (20%)
  waiting for transfers between devices  5.89 us (8%)
  other arithmetic  5.73 us (8%)
    unnamed x27, local copies, waits for them, and re-layouts  14.5 us
    dot_general x1, matrix products, to_cells(): jnp.einsum('cne,flne->flce', weighted, gll_state, precision=lax.Precision...  7.51 us
    all_to_all x1, starting transfers between devices, switch_the_inputs(): lax.all_to_all(jnp.stack(jnp.split(block_in, lax.axis_size('grp'), axis=a...  7.28 us
    all_to_all x1, starting transfers between devices, on_device(): lax.all_to_all(phys_rate.reshape(level_count, grp_size, capacity), 'grp',...  6 us
    dot_general x1, matrix products, to_nodes(): jnp.einsum('nk,flke->flne', slope_weights, neighbour_means - own_mean[:,...  3.44 us
    all_to_all x1, waiting for transfers between devices, on_device(): lax.all_to_all(phys_rate.reshape(level_count, grp_size, capacity), 'grp',...  3.24 us
    dot_general x1, matrix products, to_nodes(): jnp.einsum('nc,flce->flne', cell_to_node, tendency, precision=lax.Precisi...  2.87 us
    ppermute x1, waiting for transfers between devices, padded_2(): lax.ppermute(tail, axis, [(i, (i + 1) % count) for i in range(count)])  2.65 us
  transfers between devices with their start and end apart: 4, of which 2 were waited for; matrix products, arithmetic and copies ran while one was open for 41% of the time, Pallas kernels for 0%

profile of v1, /device:TPU:0, one launch (start us, length us, event | category | flops | bytes accessed | tf_op | source)
XLA Modules:
  0.0 70.5 jit_solution(3568819752182827030)
XLA Ops:
  0.0 1.0 %copy.133 = f32[4,8,8,128]{3,2,1,0:T(8,128)S(1)} copy(f32[4,8,8,128]{3,1,2,0:T(8,128)} %bitcast.95) | data formatting | bytes 262144
  1.1 0.6 constant_dynamic-update-slice_fusion.7
  2.9 0.6 constant_dynamic-update-slice_fusion.4
  3.5 0.6 constant_dynamic-update-slice_fusion.3
  5.9 7.3 %all-to-all-start.1 = ((f32[8,32,1,128]{3,1,2,0:T(8,128)}), f32[8,32,1,128]{3,1,2,0:T(8,128)S(1)}, u32[]{:S(2)}, u32[]{:S(2)}) async-start(f32[8,32,1,128]{3,1,2,0:T(8,128)} %constant_dynamic-update-slice_fusion), calls=%async_computation.1 | async-start | bytes 262144 | tf_op jit(solution)/shard_map/all_to_all | solution.py:12
  13.2 0.7 broadcast_multiply_fusion.1
  13.8 0.8 %copy.104 = s32[128,4,1]{1,0,2:T(8,128)S(1)} copy(s32[128,4,1]{0,2,1:T(1,128)} %param.12) | data formatting | bytes 4096 | tf_op args[2]
  14.9 8.4 %copy.108 = f32[8,32,16,128]{1,2,0,3:T(8,128)} copy(f32[8,32,16,128]{3,2,1,0:T(8,128)} %param.10) | data formatting | bytes 4194304 | tf_op args[0]
  23.6 1.1 %reduce-window.6 = s32[8,4,128]{2,0,1:T(8,128)S(1)} reduce-window(s32[8,4,128]{2,0,1:T(8,128)S(1)} %fusion.10, s32[]{:T(128)} %constant.29.clone.1), window={size=1x1x128 pad=0_0x0_0x127_0}, to_apply=%region_0.0 | reduce-window | flops 520192 | bytes 32772 | tf_op jit(solution)/shard_map/reduce-window
  25.2 7.5 %divide_bitcast_fusion = f32[8,32,128,4]{1,3,0,2:T(4,128)} fusion(f32[8,32,16,128]{1,2,0,3:T(8,128)} %copy.108, f32[128,4]{1,0:T(8,128)S(1)} %bitcast.104, f32[16,128]{0,1:T(8,128)S(1)} %copy.107, f32[4,16]{1,0:T(4,128)S(1)} %copy-done.5), kind=kOutput, calls=%fused_computation.4 | convolution fusion | flops 25305088 | bytes 2631936 | tf_op jit(solution)/shard_map/cne,flne->flce/dot_general | solution.py:85
  32.9 0.6 copy_bitcast_fusion
  33.5 6.0 %all-to-all-start = ((f32[32,8,128]{2,0,1:T(8,128)}), f32[32,8,128]{2,0,1:T(8,128)S(1)}, u32[]{:S(2)}, u32[]{:S(2)}) async-start(f32[32,8,128]{2,0,1:T(8,128)} %copy_bitcast_fusion), calls=%async_computation | async-start | bytes 262144 | tf_op jit(solution)/shard_map/all_to_all | solution.py:129
  39.5 1.8 %copy.109 = f32[8,32,128,4]{1,0,3,2:T(8,128)S(1)} copy(f32[8,32,128,4]{1,3,0,2:T(4,128)} %divide_bitcast_fusion) | data formatting | bytes 1048576 | tf_op jit(solution)/shard_map/div | solution.py:86
  41.3 0.9 %copy.110 = f32[8,32,512]{2,0,1:T(8,128)S(1)} copy(f32[8,32,512]{1,0,2:T(8,128)S(1)} %bitcast.83) | data formatting | bytes 1048576 | tf_op jit(solution)/shard_map/reshape | solution.py:119
  42.5 1.0 %gather_fusion.1 = f32[512,32]{1,0:T(8,128)S(1)} fusion(f32[32,1024]{0,1:T(8,128)S(1)} %bitcast.87, s32[1024]{0:T(1024)S(1)} %pad_clamp_fusion.1), kind=kCustom, calls=%fused_computation.1 | custom fusion | bytes 133120 | tf_op jit(solution)/shard_map/gather | solution.py:139
  43.6 3.2 %all-to-all-done = f32[32,8,128]{2,0,1:T(8,128)S(1)} async-done(((f32[32,8,128]{2,0,1:T(8,128)}), f32[32,8,128]{2,0,1:T(8,128)S(1)}, u32[]{:S(2)}, u32[]{:S(2)}) %all-to-all-start) | async-done | bytes 131104 | tf_op jit(solution)/shard_map/all_to_all | solution.py:129
  47.1 1.0 %gather_fusion = f32[512,32]{1,0:T(8,128)S(1)} fusion(f32[32,1024]{0,1:T(8,128)S(1)} %bitcast.85, s32[1024]{0:T(1024)S(1)} %pad_clamp_fusion.1), kind=kCustom, calls=%fused_computation | custom fusion | bytes 133120 | tf_op jit(solution)/shard_map/gather | solution.py:138
  48.2 0.6 fusion.2
  48.8 0.8 %copy.113 = f32[8,32,512]{1,0,2:T(8,128)S(1)} copy(f32[8,32,512]{2,0,1:T(8,128)S(1)} %fusion.2) | data formatting | bytes 1048576 | tf_op jit(solution)/shard_map/mul | solution.py:93
  49.7 1.7 %bitcast_reduce_fusion.2 = (f32[8,32,128]{1,0,2:T(8,128)S(1)}, f32[8,32,128]{1,0,2:T(8,128)}, f32[8,32,128]{1,0,2:T(8,128)S(1)}) fusion(f32[8,32,512]{1,0,2:T(8,128)S(1)} %copy.113), kind=kLoop, calls=%fused_computation.49 | loop fusion | flops 294912 | bytes 917504 | tf_op jit(solution)/shard_map/reduce_max | solution.py:109
  51.3 2.1 %copy.125 = f32[8,32,4,128]{3,2,1,0:T(4,128)} copy(f32[8,32,4,128]{1,0,2,3:T(8,128)S(1)} %bitcast.82) | data formatting | bytes 1048576 | tf_op jit(solution)/shard_map/transpose | solution.py:141
  53.4 1.2 %copy.114 = f32[8,32,128]{2,1,0:T(8,128)S(1)} copy(f32[8,32,128]{1,0,2:T(8,128)} %get-tuple-element.6) | data formatting | bytes 262144 | tf_op jit(solution)/shard_map/reduce_sum | solution.py:142
  54.7 0.6 fusion.13
  55.4 0.8 %collective-permute-start.1 = (f32[256,32]{0,1:T(8,128)}, f32[256,32]{0,1:T(8,128)}, u32[]{:S(2)}, u32[]{:S(2)}) collective-permute-start(f32[256,32]{0,1:T(8,128)} %get-tuple-element.13), channel_id=1, source_target_pairs={{1,0},{2,1},{3,2},{4,3},{5,4},{6,5},{7,6},{8,7},{9,8},{10,9},{11,1... | collective-permute-start | bytes 98312 | tf_op jit(solution)/shard_map/ppermute | solution.py:28
  56.1 2.9 %fusion.15 = f32[8,32,128,16]{2,3,1,0:T(8,128)S(1)} fusion(f32[8,32,4,128]{3,2,1,0:T(4,128)} %copy.125, f32[16,4,1,1]{0,1,3,2:T(4,128)S(1)} %copy-done.7), kind=kOutput, calls=%fused_computation.52 | convolution fusion | flops 25165824 | bytes 2621696 | tf_op jit(solution)/shard_map/nc,flce->flne/dot_general | solution.py:99
  59.0 0.9 %copy.124 = f32[8,32,128]{2,1,0:T(8,128)} copy(f32[8,32,128]{1,0,2:T(8,128)S(1)} %get-tuple-element.7) | data formatting | bytes 262144 | tf_op jit(solution)/shard_map/reduce_min | solution.py:108
  59.9 0.8 %copy.121 = f32[8,32,128]{2,1,0:T(8,128)} copy(f32[8,32,128]{1,0,2:T(8,128)S(1)} %get-tuple-element.5) | data formatting | bytes 262144 | tf_op jit(solution)/shard_map/reduce_max | solution.py:109
  60.7 2.6 %collective-permute-done = f32[256,32]{0,1:T(8,128)} collective-permute-done((f32[256,32]{0,1:T(8,128)}, f32[256,32]{0,1:T(8,128)}, u32[]{:S(2)}, u32[]{:S(2)}) %collective-permute-start) | collective-permute-done | bytes 32800 | tf_op jit(solution)/shard_map/ppermute | solution.py:26
  63.4 0.8 %pad_maximum_fusion = f32[256,192]{0,1:T(8,128)S(1)} fusion(f32[256,32]{0,1:T(8,128)} %collective-permute-done.1, f32[256,128]{0,1:T(8,128)S(1)} %copy.115, f32[256,32]{0,1:T(8,128)} %collective-permute-done), kind=kLoop, calls=%fused_computation.16 | loop fusion | flops 98304 | bytes 393216 | tf_op jit(solution)/shard_map/concatenate | solution.py:24
  64.2 1.6 %gather_fusion.2 = f32[512,256]{1,0:T(8,128)S(1)} fusion(f32[256,192]{0,1:T(8,128)S(1)} %pad_maximum_fusion, s32[1024]{0:T(1024)S(1)} %pad_clamp_fusion), kind=kCustom, calls=%fused_computation.2 | custom fusion | bytes 1050624 | tf_op jit(solution)/shard_map/jit(_take)/gather | solution.py:147
  66.1 0.9 %min.23 = f32[8,32,128]{2,1,0:T(8,128)S(1)} minimum(f32[8,32,128]{2,1,0:T(8,128)} %copy.124, f32[8,32,128]{2,1,0:T(8,128)S(1)} %bitcast.92) | non-fusion elementwise | flops 32768 | bytes 393216 | tf_op jit(solution)/shard_map/min | solution.py:108
  67.1 3.4 %minimum_bitcast_fusion = f32[8,32,16,128]{3,2,1,0:T(8,128)} fusion(f32[8,32,128,16]{2,3,1,0:T(8,128)S(1)} %fusion.15, f32[16,4,1,1]{0,1,3,2:T(4,128)S(1)} %copy-done.4, f32[8,32,128]{2,1,0:T(8,128)S(1)} %min.23, f32[8,32,128]{2,1,0:T(8,128)S(1)} %max.20, f32[8,32,4,128]{3,1,0,2:T(8,128)S(1)} %select_subtract_fusion), kind=kOutput, calls=%fused_computation.3 | convolution fusion | flops 26738688 | bytes 4980992 | tf_op jit(solution)/shard_map/nk,flke->flne/dot_general | solution.py:102
  (50 shorter events, 5.3 us)
Async XLA Ops:
  0.0 32.9 %copy-start = (f32[32,1024]{1,0:T(8,128)S(1)}, f32[32,1024]{1,0:T(8,128)}, u32[]{:S(2)}) copy-start(f32[32,1024]{1,0:T(8,128)} %param.14) | copy-start | bytes 393220
  5.9 27.6 %all-to-all-start.1 = ((f32[8,32,1,128]{3,1,2,0:T(8,128)}), f32[8,32,1,128]{3,1,2,0:T(8,128)S(1)}, u32[]{:S(2)}, u32[]{:S(2)}) async-start(f32[8,32,1,128]{3,1,2,0:T(8,128)} %constant_dynamic-update-slice_fusion), calls=%async_computation.1 | async-start | bytes 262144 | tf_op jit(solution)/shard_map/all_to_all | solution.py:12
  14.8 8.4 %copy-start.2 = (f32[16,128]{1,0:T(8,128)S(1)}, f32[16,128]{1,0:T(8,128)}, u32[]{:S(2)}) copy-start(f32[16,128]{1,0:T(8,128)} %param.11) | copy-start | bytes 24580
  14.9 10.1 %copy-start.5 = (f32[4,16]{1,0:T(4,128)S(1)}, f32[4,16]{1,0:T(4,128)}, u32[]{:S(2)}) copy-start(f32[4,16]{1,0:T(4,128)} %constant.69.clone) | copy-start | bytes 772
  25.2 14.3 %copy-start.6 = (s32[4,128]{1,0:T(4,128)S(1)}, s32[4,128]{1,0:T(4,128)}, u32[]{:S(2)}) copy-start(s32[4,128]{1,0:T(4,128)} %param.13) | copy-start | bytes 6148
  33.5 13.3 %all-to-all-start = ((f32[32,8,128]{2,0,1:T(8,128)}), f32[32,8,128]{2,0,1:T(8,128)S(1)}, u32[]{:S(2)}, u32[]{:S(2)}) async-start(f32[32,8,128]{2,0,1:T(8,128)} %copy_bitcast_fusion), calls=%async_computation | async-start | bytes 262144 | tf_op jit(solution)/shard_map/all_to_all | solution.py:129
  42.2 6.0 %copy-start.3 = (f32[8,8]{1,0:T(8,128)S(1)}, f32[8,8]{1,0:T(8,128)}, u32[]{:S(2)}) copy-start(f32[8,8]{1,0:T(8,128)} %param.16) | copy-start | bytes 772
  51.3 4.8 %copy-start.7 = (f32[16,4,1,1]{0,1,3,2:T(4,128)S(1)}, f32[16,4,1,1]{0,1,3,2:T(4,128)}, u32[]{:S(2)}) copy-start(f32[16,4,1,1]{0,1,3,2:T(4,128)} %constant.72) | copy-start | bytes 772
  55.4 5.4 %collective-permute-start.1 = (f32[256,32]{0,1:T(8,128)}, f32[256,32]{0,1:T(8,128)}, u32[]{:S(2)}, u32[]{:S(2)}) collective-permute-start(f32[256,32]{0,1:T(8,128)} %get-tuple-element.13), channel_id=1, source_target_pairs={{1,0},{2,1},{3,2},{4,3},{5,4},{6,5},{7,6},{8,7},{9,8},{10,9},{11,1... | collective-permute-start | bytes 98312 | tf_op jit(solution)/shard_map/ppermute | solution.py:28
  56.1 7.3 %collective-permute-start = (f32[256,32]{0,1:T(8,128)}, f32[256,32]{0,1:T(8,128)}, u32[]{:S(2)}, u32[]{:S(2)}) collective-permute-start(f32[256,32]{0,1:T(8,128)} %get-tuple-element.12), channel_id=1, source_target_pairs={{0,1},{1,2},{2,3},{3,4},{4,5},{5,6},{6,7},{7,8},{8,9},{9,10},{10,1... | collective-permute-start | bytes 98312 | tf_op jit(solution)/shard_map/ppermute | solution.py:26
  65.7 1.3 %copy-start.1 = (f32[8,32,128]{2,1,0:T(8,128)S(1)}, f32[8,32,128]{2,1,0:T(8,128)}, u32[]{:S(2)}) copy-start(f32[8,32,128]{2,1,0:T(8,128)} %copy.121) | copy-start | bytes 393220
  65.8 1.3 %copy-start.4 = (f32[16,4,1,1]{0,1,3,2:T(4,128)S(1)}, f32[16,4,1,1]{0,1,3,2:T(4,128)}, u32[]{:S(2)}) copy-start(f32[16,4,1,1]{0,1,3,2:T(4,128)} %constant.73) | copy-start | bytes 772
